TPU v7x, 32 devices: a whole 2x2x4 slice. The times are simulated.
32 devices in a mesh: groups: 2 (over y), slab: 4 (over z), pencil: 2 (over x), comp: 2 (over core).
Axes of the slice: x: 2, y: 2, z: 4, core: 2. Of those that a mesh axis runs over, the one named last changes fastest.
Arguments:
- u_start: float32 [3, 64, 64, 512], P(None, ('groups', 'slab'), 'pencil', 'comp'), parts along dimension 1, may hold values from -6 to 6
- toughness: float32 [64, 64, 512], P(('groups', 'slab'), 'pencil', 'comp'), parts along dimension 0, may hold values from 0.3 to 1.5
- crack_label: int32 [64, 64, 512], P(('groups', 'slab'), 'pencil', 'comp'), parts along dimension 0, may hold values from 0 to 2
- obs_weight: bfloat16 [32, 64, 2, 4096], P('slab', 'pencil', 'comp'), may hold values from -0.75 to 0.75
- sensor_cell: int32 [4096], replicated, may hold values from 0 to 4095
Outputs:
- moved: float32 [3, 64, 64, 512], P(None, ('groups', 'slab'), 'pencil', 'comp'), parts along dimension 1
- damage: float32 [64, 64, 512], P(('groups', 'slab'), 'pencil', 'comp'), parts along dimension 0
- readings: float32 [3, 8192], P(None, 'groups'), parts along dimension 1
There are 2 independent parts, one for each index of `groups`. A program takes and returns all parts, laid end to end along the dimension named above; an argument that names none is the same for every part. Nothing has to cross between parts.
Inputs may be any that keep to these rules, and one draw needn't show every extreme that they name: `sensor_cell`: numbers cell blocks as (64 z + y) * 2 + h. `crack_label`: 0 intact, 1 partly cracked, 2 cracked.
All inputs are finite; a program needn't handle non-finite values.
Results may differ from a plain program's by a relative error of at most 0.003.
Values sent between devices are 32-bit elements; how exact they have to be, the bound alone decides.
A program may use at most 128 MiB of HBM per device.

v0:
```python
import jax
import jax.numpy as jnp
from jax import lax
from jax.sharding import PartitionSpec as P

SHEAR_MODULUS = 1.0
LAME_FIRST = 1.5
RESIDUAL_STIFF = 0.001
TIME_DISP = 0.15
TIME_DAMAGE = 0.08
LENGTH_SCALE = 1.0
DAMAGE_LEVEL = 0.45
POINT_GAIN = 8.0


def with_halo(block, sides, width):
    for axis, dim in sides:
        count = lax.axis_size(axis)
        forward = [(i, i + 1) for i in range(count - 1)]
        backward = [(target, source) for source, target in forward]
        low = lax.ppermute(
            lax.slice_in_dim(block, block.shape[dim] - width, None, axis=dim), axis, forward
        )
        high = lax.ppermute(lax.slice_in_dim(block, 0, width, axis=dim), axis, backward)
        block = jnp.concatenate([low, block, high], axis=dim)
    return block


def central(source, spatial):
    if spatial == 0:
        return 0.5 * (source[..., 2:, 1:-1, 1:-1] - source[..., :-2, 1:-1, 1:-1])
    if spatial == 1:
        return 0.5 * (source[..., 1:-1, 2:, 1:-1] - source[..., 1:-1, :-2, 1:-1])
    return 0.5 * (source[..., 1:-1, 1:-1, 2:] - source[..., 1:-1, 1:-1, :-2])


def shrink(source):
    return source[..., 1:-1, 1:-1, 1:-1]


def laplace(source):
    return (
        source[2:, 1:-1, 1:-1]
        + source[:-2, 1:-1, 1:-1]
        + source[1:-1, 2:, 1:-1]
        + source[1:-1, :-2, 1:-1]
        + source[1:-1, 1:-1, 2:]
        + source[1:-1, 1:-1, :-2]
        - 6.0 * source[1:-1, 1:-1, 1:-1]
    )


def entry_key(first, second):
    return (min(first, second), max(first, second))


def rotate(matrix, first, second):
    other = 3 - first - second
    diag_first = matrix[first, first]
    diag_second = matrix[second, second]
    coupling = matrix[first, second]
    angle = 0.5 * jnp.arctan2(2.0 * coupling, diag_second - diag_first)
    cosine = jnp.cos(angle)
    sine = jnp.sin(angle)
    side_first = matrix[entry_key(other, first)]
    side_second = matrix[entry_key(other, second)]
    result = dict(matrix)
    result[first, first] = (
        cosine * cosine * diag_first - 2.0 * cosine * sine * coupling + sine * sine * diag_second
    )
    result[second, second] = (
        sine * sine * diag_first + 2.0 * cosine * sine * coupling + cosine * cosine * diag_second
    )
    result[first, second] = jnp.zeros_like(coupling)
    result[entry_key(other, first)] = cosine * side_first - sine * side_second
    result[entry_key(other, second)] = sine * side_first + cosine * side_second
    return result


def eigenvalues(matrix):
    for sweep_index in range(5):
        for first, second in ((0, 1), (0, 2), (1, 2)):
            matrix = rotate(matrix, first, second)
    return [matrix[0, 0], matrix[1, 1], matrix[2, 2]]


def advance(padded_disp, padded_damage, toughness):
    gradient = [
        [central(padded_disp[component], direction) for direction in range(3)]
        for component in range(3)
    ]
    strain = {}
    for first in range(3):
        for second in range(first, 3):
            strain[first, second] = 0.5 * (gradient[first][second] + gradient[second][first])
    trace_full = strain[0, 0] + strain[1, 1] + strain[2, 2]
    damage_mid = shrink(padded_damage)
    degrade = (1.0 - damage_mid) ** 2 + RESIDUAL_STIFF
    divergence = []
    for component in range(3):
        total_force = 0.0
        for direction in range(3):
            stress = 2.0 * SHEAR_MODULUS * strain[entry_key(component, direction)]
            if component == direction:
                stress = stress + LAME_FIRST * trace_full
            total_force = total_force + central(degrade * stress, direction)
        divergence.append(total_force)
    moved = shrink(shrink(padded_disp)) + TIME_DISP * jnp.stack(divergence)
    inner = {key_pair: shrink(entry_value) for key_pair, entry_value in strain.items()}
    trace_inner = shrink(trace_full)
    energy = 0.5 * LAME_FIRST * jnp.maximum(trace_inner, 0.0) ** 2
    for eigen_value in eigenvalues(inner):
        energy = energy + SHEAR_MODULUS * jnp.maximum(eigen_value, 0.0) ** 2
    damage_core = shrink(damage_mid)
    damage = damage_core + TIME_DAMAGE * (
        2.0 * (1.0 - damage_core) * energy
        - toughness / LENGTH_SCALE * damage_core
        + toughness * LENGTH_SCALE * laplace(damage_mid)
    )
    return (moved, damage)


def local(u_start, toughness, crack_label, obs_weight, sensor_cell):
    planes, rows, columns = toughness.shape
    damage = DAMAGE_LEVEL * crack_label.astype(jnp.float32)
    moved = u_start
    for repeat in range(2):
        stacked = jnp.concatenate([moved, damage[None]], axis=0)
        padded = with_halo(stacked, (("slab", 1), ("pencil", 2), ("comp", 3)), 2)
        moved, damage = advance(padded[:3], padded[3], toughness)
    pooled = jnp.mean(moved, axis=-1).reshape(3, planes * rows).astype(jnp.bfloat16)
    weight_rows = obs_weight.reshape(planes * rows, obs_weight.shape[-1])
    dense = jnp.dot(pooled, weight_rows, preferred_element_type=jnp.float32)
    plane_ids = lax.axis_index("slab") * planes + jnp.arange(planes, dtype=jnp.int32)
    row_ids = lax.axis_index("pencil") * rows + jnp.arange(rows, dtype=jnp.int32)
    block_ids = (
        (plane_ids[:, None] * (rows * lax.axis_size("pencil")) + row_ids[None, :])
        * lax.axis_size("comp")
        + lax.axis_index("comp")
    ).reshape(planes * rows)
    picks = (block_ids[:, None] == sensor_cell[None, :]).astype(jnp.bfloat16)
    point = jnp.dot(pooled, picks, preferred_element_type=jnp.float32)
    partial_sum = dense + POINT_GAIN * point
    readings = lax.psum(partial_sum, ("slab", "pencil", "comp"))
    return (moved, damage, readings)


def solution(mesh):
    return jax.shard_map(
        local,
        mesh=mesh,
        in_specs=(
            P(None, ("groups", "slab"), "pencil", "comp"),
            P(("groups", "slab"), "pencil", "comp"),
            P(("groups", "slab"), "pencil", "comp"),
            P("slab", "pencil", "comp", None),
            P(),
        ),
        out_specs=(
            P(None, ("groups", "slab"), "pencil", "comp"),
            P(("groups", "slab"), "pencil", "comp"),
            P(None, "groups"),
        ),
        check_vma=False,
    )
```

profile of v0, /device:TPU:0, one launch (start us, length us, event | category | flops | bytes accessed | tf_op | source)
XLA Modules:
  0.0 226.6 jit_solution(18250146474018214217)
XLA Ops:
  2.9 5.0 %collective-permute-start = (f32[4,2,32,256]{3,2,1,0:T(8,128)S(1)}, f32[4,2,32,256]{3,2,1,0:T(8,128)S(1)}, u32[]{:S(2)}, u32[]{:S(2)}) collective-permute-start(f32[4,2,32,256]{3,2,1,0:T(8,128)S(1)} %get-tuple-element.66), channel_id=1, source_target_pairs={{0,4},{4,8},{8,12},{1,5},{5,9},{9,13},{2,6},{6,10},{10,14},{3,7},{... | collective-permute-start | bytes 786440 | tf_op jit(solution)/shard_map/ppermute | solution.py:21
  9.1 4.2 %collective-permute-done = f32[4,2,32,256]{3,2,1,0:T(8,128)S(1)} collective-permute-done((f32[4,2,32,256]{3,2,1,0:T(8,128)S(1)}, f32[4,2,32,256]{3,2,1,0:T(8,128)S(1)}, u32[]{:S(2)}, u32[]{:S(2)}) %collective-permute-start) | collective-permute-done | bytes 262176 | tf_op jit(solution)/shard_map/ppermute | solution.py:21
  13.4 4.1 %collective-permute-done.1 = f32[4,2,32,256]{3,2,1,0:T(8,128)S(1)} collective-permute-done((f32[4,2,32,256]{3,2,1,0:T(8,128)S(1)}, f32[4,2,32,256]{3,2,1,0:T(8,128)S(1)}, u32[]{:S(2)}, u32[]{:S(2)}) %collective-permute-start.1) | collective-permute-done | bytes 262176 | tf_op jit(solution)/shard_map/ppermute | solution.py:24
  18.7 3.4 %collective-permute-start.2 = (f32[4,12,2,256]{3,2,1,0:T(2,128)S(1)}, f32[4,12,2,256]{3,2,1,0:T(2,128)S(1)}, u32[]{:S(2)}, u32[]{:S(2)}) collective-permute-start(f32[4,12,2,256]{3,2,1,0:T(2,128)S(1)} %get-tuple-element.58), channel_id=1, source_target_pairs={{0,2},{1,3},{4,6},{5,7},{8,10},{9,11},{12,14},{13,15},{16,18},{17,... | collective-permute-start | bytes 294920 | tf_op jit(solution)/shard_map/ppermute | solution.py:21
  24.3 4.3 %collective-permute-done.3 = f32[4,12,2,256]{3,2,1,0:T(2,128)S(1)} collective-permute-done((f32[4,12,2,256]{3,2,1,0:T(2,128)S(1)}, f32[4,12,2,256]{3,2,1,0:T(2,128)S(1)}, u32[]{:S(2)}, u32[]{:S(2)}) %collective-permute-start.3) | collective-permute-done | bytes 98336 | tf_op jit(solution)/shard_map/ppermute | solution.py:24
  34.1 2.2 copy.25
  37.6 2.2 copy.26
  39.8 2.2 copy.27
  42.0 3.1 %pad_maximum_fusion = f32[4,12,36,260]{3,2,1,0:T(8,128)S(1)} fusion(f32[4,12,36,2]{3,2,1,0:T(8,128)} %copy.27, f32[4,12,2,256]{3,2,1,0:T(2,128)} %copy-done.13, f32[4,2,32,256]{3,2,1,0:T(8,128)} %copy-done.5, f32[1,8,32,256]{3,2,1,0:T(8,128)S(1)} %multiply_bitcast_fusion, f32[3,8,32,256]{3,2,1,0:T(8,128)S(1)} %copy-done.1, ...), kind=kLoop, calls=%fused_computation.3 | loop fusion | flops 3144960 | bytes 3594240 | tf_op jit(solution)/shard_map/concatenate | solution.py:25
  45.3 2.2 multiply_multiply_fusion.5
  50.1 29.3 %fusion.51 = f32[1,8,32,256]{3,2,1,0:T(8,128)S(1)} fusion(f32[8,32,256]{2,1,0:T(8,128)S(1)} %copy-done.15, f32[12,36,260]{2,1,0:T(8,128)S(1)} %get-tuple-element.37, f32[10,34,258]{2,1,0:T(8,128)S(1)} %get-tuple-element.46, f32[10,34,258]{2,1,0:T(8,128)S(1)} %get-tuple-element.47, f32[10,34,258]{2,1,0:T(8,128)S(1)} %get-tuple-element.29, ...), kind=kLoop, calls=%fused_computation.127 | loop fusion | flops 23068672 | bytes 4194304 | tf_op jit(solution)/shard_map/broadcast_in_dim | solution.py:128
  80.3 3.5 %collective-permute-start.6 = (f32[4,2,32,256]{3,2,1,0:T(8,128)}, f32[4,2,32,256]{3,2,1,0:T(8,128)S(1)}, u32[]{:S(2)}, u32[]{:S(2)}) collective-permute-start(f32[4,2,32,256]{3,2,1,0:T(8,128)} %get-tuple-element.64), channel_id=1, source_target_pairs={{0,4},{4,8},{8,12},{1,5},{5,9},{9,13},{2,6},{6,10},{10,14},{3,7},{... | collective-permute-start | bytes 786440 | tf_op jit(solution)/shard_map/ppermute | solution.py:21
  85.7 4.3 %collective-permute-done.6 = f32[4,2,32,256]{3,2,1,0:T(8,128)S(1)} collective-permute-done((f32[4,2,32,256]{3,2,1,0:T(8,128)}, f32[4,2,32,256]{3,2,1,0:T(8,128)S(1)}, u32[]{:S(2)}, u32[]{:S(2)}) %collective-permute-start.6) | collective-permute-done | bytes 262176 | tf_op jit(solution)/shard_map/ppermute | solution.py:21
  90.0 4.7 %collective-permute-done.7 = f32[4,2,32,256]{3,2,1,0:T(8,128)} collective-permute-done((f32[4,2,32,256]{3,2,1,0:T(8,128)}, f32[4,2,32,256]{3,2,1,0:T(8,128)}, u32[]{:S(2)}, u32[]{:S(2)}) %collective-permute-start.7) | collective-permute-done | bytes 262176 | tf_op jit(solution)/shard_map/ppermute | solution.py:24
  100.0 4.1 %collective-permute-done.9 = f32[4,12,2,256]{3,2,1,0:T(2,128)S(1)} collective-permute-done((f32[4,12,2,256]{3,2,1,0:T(2,128)S(1)}, f32[4,12,2,256]{3,2,1,0:T(2,128)S(1)}, u32[]{:S(2)}, u32[]{:S(2)}) %collective-permute-start.9) | collective-permute-done | bytes 98336 | tf_op jit(solution)/shard_map/ppermute | solution.py:24
  108.8 1.9 collective-permute-start.10
  110.7 2.2 copy.29
  117.0 2.2 copy.30
  119.2 2.2 copy.31
  121.4 3.3 %pad_maximum_fusion.1 = f32[4,12,36,260]{3,2,1,0:T(8,128)S(1)} fusion(f32[4,12,36,2]{3,2,1,0:T(8,128)} %copy.31, f32[4,12,2,256]{3,2,1,0:T(2,128)} %copy-done.12, f32[4,2,32,256]{3,2,1,0:T(8,128)} %collective-permute-done.7, f32[1,8,32,256]{3,2,1,0:T(8,128)S(1)} %fusion.51, f32[3,8,32,256]{3,2,1,0:T(8,128)} %copy-done.2, ...), kind=kLoop, calls=%fused_computation.4 | loop fusion | flops 3144960 | bytes 3594240 | tf_op jit(solution)/shard_map/concatenate | solution.py:25
  124.9 3.8 %multiply_multiply_fusion.2 = (f32[10,34,258]{2,1,0:T(8,128)S(1)}, f32[10,34,258]{2,1,0:T(8,128)}, f32[10,34,258]{2,1,0:T(8,128)S(1)}, f32[10,34,258]{2,1,0:T(8,...) fusion(f32[12,36,260]{2,1,0:T(8,128)S(1)} %get-tuple-element.33, ...), kind=kLoop, calls=%fused_computation.61 | loop fusion | flops 2456160 | bytes 8421120 | tf_op jit(solution)/shard_map/mul | solution.py:106
  128.7 2.1 multiply_multiply_fusion
  135.0 60.5 %psum.7 = f32[3,4096]{1,0:T(4,128)} all-reduce(f32[3,4096]{1,0:T(4,128)} %fusion), channel_id=1, replica_groups=mesh['groups'=2,'slab'=4,'pencil'=2,'comp'=2] {'slab','pencil','comp'}, use_global_device_ids=true, to_apply=%region_1.0 | all-reduce | flops 12288 | bytes 98304 | tf_op jit(solution)/shard_map/psum | solution.py:144
  195.5 31.0 %fusion.26 = f32[8,32,256]{2,1,0:T(8,128)} fusion(f32[8,32,256]{2,1,0:T(8,128)} %param.6, f32[12,36,260]{2,1,0:T(8,128)S(1)} %copy-done.4, f32[10,34,258]{2,1,0:T(8,128)S(1)} %get-tuple-element.39, f32[10,34,258]{2,1,0:T(8,128)} %get-tuple-element.40, f32[10,34,258]{2,1,0:T(8,128)} %get-tuple-element.18, f32[10,34,258]{2,1,0:T(8,128)} %get-tuple-element.44, ...), kind=kLoop, calls=%fused_computation.82 | loop fusion | flops 23068672 | bytes 4194304 | tf_op jit(solution)/shard_map/add | solution.py:115
  (74 shorter events, 37.3 us)
Async XLA Ops:
  0.6 132.5 %copy-start = (bf16[8,32,1,4096]{3,1,2,0:T(8,128)(2,1)S(1)}, bf16[8,32,1,4096]{3,1,2,0:T(8,128)(2,1)}, u32[]{:S(2)}) copy-start(bf16[8,32,1,4096]{3,1,2,0:T(8,128)(2,1)} %param.8) | copy-start | bytes 6291460
  0.6 28.0 %copy-start.1 = (f32[3,8,32,256]{3,2,1,0:T(8,128)S(1)}, f32[3,8,32,256]{3,2,1,0:T(8,128)}, u32[]{:S(2)}) copy-start(f32[3,8,32,256]{3,2,1,0:T(8,128)} %param.5) | copy-start | bytes 2359300
  2.9 10.5 %collective-permute-start = (f32[4,2,32,256]{3,2,1,0:T(8,128)S(1)}, f32[4,2,32,256]{3,2,1,0:T(8,128)S(1)}, u32[]{:S(2)}, u32[]{:S(2)}) collective-permute-start(f32[4,2,32,256]{3,2,1,0:T(8,128)S(1)} %get-tuple-element.66), channel_id=1, source_target_pairs={{0,4},{4,8},{8,12},{1,5},{5,9},{9,13},{2,6},{6,10},{10,14},{3,7},{... | collective-permute-start | bytes 786440 | tf_op jit(solution)/shard_map/ppermute | solution.py:21
  7.8 9.7 %collective-permute-start.1 = (f32[4,2,32,256]{3,2,1,0:T(8,128)S(1)}, f32[4,2,32,256]{3,2,1,0:T(8,128)S(1)}, u32[]{:S(2)}, u32[]{:S(2)}) collective-permute-start(f32[4,2,32,256]{3,2,1,0:T(8,128)S(1)} %get-tuple-element.67), channel_id=1, source_target_pairs={{4,0},{8,4},{12,8},{5,1},{9,5},{13,9},{6,2},{10,6},{14,10},{7,3},{... | collective-permute-start | bytes 786440 | tf_op jit(solution)/shard_map/ppermute | solution.py:24
  17.5 13.0 %copy-start.5 = (f32[4,2,32,256]{3,2,1,0:T(8,128)}, f32[4,2,32,256]{3,2,1,0:T(8,128)S(1)}, u32[]{:S(2)}) copy-start(f32[4,2,32,256]{3,2,1,0:T(8,128)S(1)} %collective-permute-done.1) | copy-start | bytes 786436
  18.7 5.6 %collective-permute-start.2 = (f32[4,12,2,256]{3,2,1,0:T(2,128)S(1)}, f32[4,12,2,256]{3,2,1,0:T(2,128)S(1)}, u32[]{:S(2)}, u32[]{:S(2)}) collective-permute-start(f32[4,12,2,256]{3,2,1,0:T(2,128)S(1)} %get-tuple-element.58), channel_id=1, source_target_pairs={{0,2},{1,3},{4,6},{5,7},{8,10},{9,11},{12,14},{13,15},{16,18},{17,... | collective-permute-start | bytes 294920 | tf_op jit(solution)/shard_map/ppermute | solution.py:21
  22.1 6.5 %collective-permute-start.3 = (f32[4,12,2,256]{3,2,1,0:T(2,128)S(1)}, f32[4,12,2,256]{3,2,1,0:T(2,128)S(1)}, u32[]{:S(2)}, u32[]{:S(2)}) collective-permute-start(f32[4,12,2,256]{3,2,1,0:T(2,128)S(1)} %get-tuple-element.59), channel_id=1, source_target_pairs={{2,0},{3,1},{6,4},{7,5},{10,8},{11,9},{14,12},{15,13},{18,16},{19,... | collective-permute-start | bytes 294920 | tf_op jit(solution)/shard_map/ppermute | solution.py:24
  28.6 1.9 copy-start.13
  32.2 5.4 %collective-permute-start.4 = (f32[4,12,36,2]{2,0,3,1:T(4,128)S(1)}, f32[4,12,36,2]{2,0,3,1:T(4,128)}, u32[]{:S(2)}, u32[]{:S(2)}) collective-permute-start(f32[4,12,36,2]{2,0,3,1:T(4,128)S(1)} %copy.24), channel_id=1, source_target_pairs={{0,1},{2,3},{4,5},{6,7},{8,9},{10,11},{12,13},{14,15},{16,17},{18,... | collective-permute-start | bytes 41480 | tf_op jit(solution)/shard_map/ppermute | solution.py:21
  36.3 3.5 %collective-permute-start.5 = (f32[4,12,36,2]{2,0,3,1:T(4,128)}, f32[4,12,36,2]{2,0,3,1:T(4,128)}, u32[]{:S(2)}, u32[]{:S(2)}) collective-permute-start(f32[4,12,36,2]{2,0,3,1:T(4,128)} %copy.25), channel_id=1, source_target_pairs={{1,0},{3,2},{5,4},{7,6},{9,8},{11,10},{13,12},{15,14},{17,16},{19,... | collective-permute-start | bytes 41480 | tf_op jit(solution)/shard_map/ppermute | solution.py:24
  49.9 29.5 %copy-start.6 = (f32[1,8,32,256]{3,2,1,0:T(8,128)}, f32[1,8,32,256]{3,2,1,0:T(8,128)S(1)}, u32[]{:S(2)}) copy-start(f32[1,8,32,256]{3,2,1,0:T(8,128)S(1)} %get-tuple-element.71) | copy-start | bytes 786436
  49.9 29.5 %copy-start.8 = (f32[1,8,32,256]{3,2,1,0:T(8,128)}, f32[1,8,32,256]{3,2,1,0:T(8,128)S(1)}, u32[]{:S(2)}) copy-start(f32[1,8,32,256]{3,2,1,0:T(8,128)S(1)} %get-tuple-element.72) | copy-start | bytes 786436
  50.0 29.5 %copy-start.10 = (f32[1,8,32,256]{3,2,1,0:T(8,128)}, f32[1,8,32,256]{3,2,1,0:T(8,128)S(1)}, u32[]{:S(2)}) copy-start(f32[1,8,32,256]{3,2,1,0:T(8,128)S(1)} %get-tuple-element.73) | copy-start | bytes 786436
  50.1 30.2 %copy-start.2 = (f32[3,8,32,256]{3,2,1,0:T(8,128)}, f32[3,8,32,256]{3,2,1,0:T(8,128)S(1)}, u32[]{:S(2)}) copy-start(f32[3,8,32,256]{3,2,1,0:T(8,128)S(1)} %fusion.4) | copy-start | bytes 2359300
  80.3 9.7 %collective-permute-start.6 = (f32[4,2,32,256]{3,2,1,0:T(8,128)}, f32[4,2,32,256]{3,2,1,0:T(8,128)S(1)}, u32[]{:S(2)}, u32[]{:S(2)}) collective-permute-start(f32[4,2,32,256]{3,2,1,0:T(8,128)} %get-tuple-element.64), channel_id=1, source_target_pairs={{0,4},{4,8},{8,12},{1,5},{5,9},{9,13},{2,6},{6,10},{10,14},{3,7},{... | collective-permute-start | bytes 786440 | tf_op jit(solution)/shard_map/ppermute | solution.py:21
  83.8 10.9 %collective-permute-start.7 = (f32[4,2,32,256]{3,2,1,0:T(8,128)}, f32[4,2,32,256]{3,2,1,0:T(8,128)}, u32[]{:S(2)}, u32[]{:S(2)}) collective-permute-start(f32[4,2,32,256]{3,2,1,0:T(8,128)} %get-tuple-element.65), channel_id=1, source_target_pairs={{4,0},{8,4},{12,8},{5,1},{9,5},{13,9},{6,2},{10,6},{14,10},{7,3},{... | collective-permute-start | bytes 786440 | tf_op jit(solution)/shard_map/ppermute | solution.py:24
  95.9 4.1 %collective-permute-start.8 = (f32[4,12,2,256]{3,2,1,0:T(2,128)S(1)}, f32[4,12,2,256]{3,2,1,0:T(2,128)S(1)}, u32[]{:S(2)}, u32[]{:S(2)}) collective-permute-start(f32[4,12,2,256]{3,2,1,0:T(2,128)S(1)} %get-tuple-element.56), channel_id=1, source_target_pairs={{0,2},{1,3},{4,6},{5,7},{8,10},{9,11},{12,14},{13,15},{16,18},{17,... | collective-permute-start | bytes 294920 | tf_op jit(solution)/shard_map/ppermute | solution.py:21
  97.4 6.7 %collective-permute-start.9 = (f32[4,12,2,256]{3,2,1,0:T(2,128)S(1)}, f32[4,12,2,256]{3,2,1,0:T(2,128)S(1)}, u32[]{:S(2)}, u32[]{:S(2)}) collective-permute-start(f32[4,12,2,256]{3,2,1,0:T(2,128)S(1)} %get-tuple-element.57), channel_id=1, source_target_pairs={{2,0},{3,1},{6,4},{7,5},{10,8},{11,9},{14,12},{15,13},{18,16},{19,... | collective-permute-start | bytes 294920 | tf_op jit(solution)/shard_map/ppermute | solution.py:24
  104.1 3.1 %copy-start.12 = (f32[4,12,2,256]{3,2,1,0:T(2,128)}, f32[4,12,2,256]{3,2,1,0:T(2,128)S(1)}, u32[]{:S(2)}) copy-start(f32[4,12,2,256]{3,2,1,0:T(2,128)S(1)} %collective-permute-done.9) | copy-start | bytes 294916
  108.8 8.1 %collective-permute-start.10 = (f32[4,12,36,2]{2,0,3,1:T(4,128)S(1)}, f32[4,12,36,2]{2,0,3,1:T(4,128)}, u32[]{:S(2)}, u32[]{:S(2)}) collective-permute-start(f32[4,12,36,2]{2,0,3,1:T(4,128)S(1)} %copy.28), channel_id=1, source_target_pairs={{0,1},{2,3},{4,5},{6,7},{8,9},{10,11},{12,13},{14,15},{16,17},{18,... | collective-permute-start | bytes 41480 | tf_op jit(solution)/shard_map/ppermute | solution.py:21
  113.0 6.2 %collective-permute-start.11 = (f32[4,12,36,2]{2,0,3,1:T(4,128)}, f32[4,12,36,2]{2,0,3,1:T(4,128)}, u32[]{:S(2)}, u32[]{:S(2)}) collective-permute-start(f32[4,12,36,2]{2,0,3,1:T(4,128)} %copy.29), channel_id=1, source_target_pairs={{1,0},{3,2},{5,4},{7,6},{9,8},{11,10},{13,12},{15,14},{17,16},{19,... | collective-permute-start | bytes 41480 | tf_op jit(solution)/shard_map/ppermute | solution.py:24
  124.9 3.8 %copy-start.3 = (f32[12,36,260]{2,1,0:T(8,128)}, f32[12,36,260]{2,1,0:T(8,128)S(1)}, u32[]{:S(2)}) copy-start(f32[12,36,260]{2,1,0:T(8,128)S(1)} %get-tuple-element.33) | copy-start | bytes 1347844
  132.0 1.6 copy-start.14
  133.1 62.5 %copy-start.4 = (f32[12,36,260]{2,1,0:T(8,128)S(1)}, f32[12,36,260]{2,1,0:T(8,128)}, u32[]{:S(2)}) copy-start(f32[12,36,260]{2,1,0:T(8,128)} %copy-done.3) | copy-start | bytes 1347844
  (5 other events, 6.4 us)
where the time goes:
time: 228 us; the launch traced here: 227 us
  other arithmetic  89.2 us (39%)
  blocking collectives  60.5 us (27%)
  waiting for transfers between devices  27.4 us (12%)
  starting transfers between devices  24.9 us (11%)
  local copies, waits for them, and re-layouts  21.7 us (10%)
    psum x1, blocking collectives, local(): readings = lax.psum(partial_sum, ('slab', 'pencil', 'comp'))  60.5 us
    add x1, other arithmetic, advance(): damage_core + TIME_DAMAGE * (2.0 * (1.0 - damage_core) * energy - toughne...  31 us
    broadcast_in_dim x2, other arithmetic, local(): stacked = jnp.concatenate([moved, damage[None]], axis=0)  30.5 us
    ppermute x6, waiting for transfers between devices, with_halo(): lax.ppermute(lax.slice_in_dim(block, 0, width, axis=dim), axis, backward)  17.3 us
    ppermute x6, starting transfers between devices, with_halo(): lax.ppermute(lax.slice_in_dim(block, block.shape[dim] - width, None, axis...  17.2 us
    ppermute x6, waiting for transfers between devices, with_halo(): lax.ppermute(lax.slice_in_dim(block, block.shape[dim] - width, None, axis...  10.2 us
    mul x4, other arithmetic, advance(): total_force = total_force + central(degrade * stress, direction)  9.3 us
    concatenate x4, other arithmetic, with_halo(): block = jnp.concatenate([low, block, high], axis=dim)  8.23 us
  transfers between devices with their start and end apart: 12, of which 8 were waited for; matrix products, arithmetic and copies ran while one was open for 6% of the time, Pallas kernels for 0%

commit v1 on v0

--- a/solution.py
+++ b/solution.py
@@ -2,6 +2,7 @@
 import jax.numpy as jnp
 from jax import lax
 from jax.sharding import PartitionSpec as P
+from jax.lax import psum
 
 SHEAR_MODULUS = 1.0
 LAME_FIRST = 1.5
@@ -141,7 +142,7 @@
     picks = (block_ids[:, None] == sensor_cell[None, :]).astype(jnp.bfloat16)
     point = jnp.dot(pooled, picks, preferred_element_type=jnp.float32)
     partial_sum = dense + POINT_GAIN * point
-    readings = lax.psum(partial_sum, ("slab", "pencil", "comp"))
+    readings = psum(psum(partial_sum, ("pencil", "comp")), "slab")
     return (moved, damage, readings)
 
 

time: 228 us -> 199 us (0.87)
  blocking collectives: 60.5 us -> 32.4 us
    psum x1 -> x2, blocking collectives: 60.5 us -> 32.4 us  [local(): readings = psum(psum(partial_sum, ('pencil', 'comp')), 'slab')]
where the time goes in v1:
time: 199 us; the launch traced here: 198 us
  other arithmetic  89.2 us (45%)
  blocking collectives  32.4 us (16%)
  waiting for transfers between devices  27.4 us (14%)
  starting transfers between devices  24.9 us (13%)
  local copies, waits for them, and re-layouts  21.6 us (11%)
    psum x2, blocking collectives, local(): readings = psum(psum(partial_sum, ('pencil', 'comp')), 'slab')  32.4 us
    add x1, other arithmetic, advance(): damage_core + TIME_DAMAGE * (2.0 * (1.0 - damage_core) * energy - toughne...  31 us
    broadcast_in_dim x2, other arithmetic, local(): stacked = jnp.concatenate([moved, damage[None]], axis=0)  30.5 us
    ppermute x6, waiting for transfers between devices, with_halo(): lax.ppermute(lax.slice_in_dim(block, 0, width, axis=dim), axis, backward)  17.3 us
    ppermute x6, starting transfers between devices, with_halo(): lax.ppermute(lax.slice_in_dim(block, block.shape[dim] - width, None, axis...  17.2 us
    ppermute x6, waiting for transfers between devices, with_halo(): lax.ppermute(lax.slice_in_dim(block, block.shape[dim] - width, None, axis...  10.2 us
    mul x4, other arithmetic, advance(): total_force = total_force + central(degrade * stress, direction)  9.29 us
    concatenate x4, other arithmetic, with_halo(): block = jnp.concatenate([low, block, high], axis=dim)  8.23 us
  transfers between devices with their start and end apart: 12, of which 8 were waited for; matrix products, arithmetic and copies ran while one was open for 6% of the time, Pallas kernels for 0%

profile of v1, /device:TPU:0, one launch (start us, length us, event | category | flops | bytes accessed | tf_op | source)
XLA Modules:
  0.0 198.3 jit_solution(6392103848237153128)
XLA Ops:
  2.9 5.0 %collective-permute-start = (f32[4,2,32,256]{3,2,1,0:T(8,128)S(1)}, f32[4,2,32,256]{3,2,1,0:T(8,128)S(1)}, u32[]{:S(2)}, u32[]{:S(2)}) collective-permute-start(f32[4,2,32,256]{3,2,1,0:T(8,128)S(1)} %get-tuple-element.66), channel_id=1, source_target_pairs={{0,4},{4,8},{8,12},{1,5},{5,9},{9,13},{2,6},{6,10},{10,14},{3,7},{... | collective-permute-start | bytes 786440 | tf_op jit(solution)/shard_map/ppermute | solution.py:22
  9.1 4.2 %collective-permute-done = f32[4,2,32,256]{3,2,1,0:T(8,128)S(1)} collective-permute-done((f32[4,2,32,256]{3,2,1,0:T(8,128)S(1)}, f32[4,2,32,256]{3,2,1,0:T(8,128)S(1)}, u32[]{:S(2)}, u32[]{:S(2)}) %collective-permute-start) | collective-permute-done | bytes 262176 | tf_op jit(solution)/shard_map/ppermute | solution.py:22
  13.4 4.1 %collective-permute-done.1 = f32[4,2,32,256]{3,2,1,0:T(8,128)S(1)} collective-permute-done((f32[4,2,32,256]{3,2,1,0:T(8,128)S(1)}, f32[4,2,32,256]{3,2,1,0:T(8,128)S(1)}, u32[]{:S(2)}, u32[]{:S(2)}) %collective-permute-start.1) | collective-permute-done | bytes 262176 | tf_op jit(solution)/shard_map/ppermute | solution.py:25
  18.7 3.4 %collective-permute-start.2 = (f32[4,12,2,256]{3,2,1,0:T(2,128)S(1)}, f32[4,12,2,256]{3,2,1,0:T(2,128)S(1)}, u32[]{:S(2)}, u32[]{:S(2)}) collective-permute-start(f32[4,12,2,256]{3,2,1,0:T(2,128)S(1)} %get-tuple-element.58), channel_id=1, source_target_pairs={{0,2},{1,3},{4,6},{5,7},{8,10},{9,11},{12,14},{13,15},{16,18},{17,... | collective-permute-start | bytes 294920 | tf_op jit(solution)/shard_map/ppermute | solution.py:22
  24.3 4.3 %collective-permute-done.3 = f32[4,12,2,256]{3,2,1,0:T(2,128)S(1)} collective-permute-done((f32[4,12,2,256]{3,2,1,0:T(2,128)S(1)}, f32[4,12,2,256]{3,2,1,0:T(2,128)S(1)}, u32[]{:S(2)}, u32[]{:S(2)}) %collective-permute-start.3) | collective-permute-done | bytes 98336 | tf_op jit(solution)/shard_map/ppermute | solution.py:25
  34.0 2.2 %copy.25 = f32[4,12,36,2]{2,0,3,1:T(4,128)} copy(f32[4,12,36,2]{3,2,1,0:T(8,128)} %get-tuple-element.55) | data formatting | bytes 27648 | tf_op jit(solution)/shard_map/slice | solution.py:25
  37.6 2.2 %copy.26 = f32[4,12,36,2]{3,2,1,0:T(8,128)} copy(f32[4,12,36,2]{2,0,3,1:T(4,128)} %collective-permute-done.4) | data formatting | bytes 27648 | tf_op jit(solution)/shard_map/ppermute | solution.py:22
  39.8 2.2 %copy.27 = f32[4,12,36,2]{3,2,1,0:T(8,128)} copy(f32[4,12,36,2]{2,0,3,1:T(4,128)} %collective-permute-done.5) | data formatting | bytes 27648 | tf_op jit(solution)/shard_map/ppermute | solution.py:25
  42.0 3.1 %pad_maximum_fusion = f32[4,12,36,260]{3,2,1,0:T(8,128)S(1)} fusion(f32[4,12,36,2]{3,2,1,0:T(8,128)} %copy.27, f32[4,12,2,256]{3,2,1,0:T(2,128)} %copy-done.13, f32[4,2,32,256]{3,2,1,0:T(8,128)} %copy-done.5, f32[1,8,32,256]{3,2,1,0:T(8,128)S(1)} %multiply_bitcast_fusion, f32[3,8,32,256]{3,2,1,0:T(8,128)S(1)} %copy-done.1, ...), kind=kLoop, calls=%fused_computation.3 | loop fusion | flops 3144960 | bytes 3594240 | tf_op jit(solution)/shard_map/concatenate | solution.py:26
  45.3 2.2 %multiply_multiply_fusion.5 = (f32[10,34,258]{2,1,0:T(8,128)S(1)}, f32[10,34,258]{2,1,0:T(8,128)S(1)}, f32[10,34,258]{2,1,0:T(8,128)S(1)}, f32[10,34,258]{2,1,0:...) fusion(f32[12,36,260]{2,1,0:T(8,128)S(1)} %get-tuple-element.37, ...), kind=kLoop, calls=%fused_computation.68 | loop fusion | flops 2456160 | bytes 8421120 | tf_op jit(solution)/shard_map/mul | solution.py:107
  50.1 29.3 %fusion.51 = f32[1,8,32,256]{3,2,1,0:T(8,128)S(1)} fusion(f32[8,32,256]{2,1,0:T(8,128)S(1)} %copy-done.15, f32[12,36,260]{2,1,0:T(8,128)S(1)} %get-tuple-element.37, f32[10,34,258]{2,1,0:T(8,128)S(1)} %get-tuple-element.46, f32[10,34,258]{2,1,0:T(8,128)S(1)} %get-tuple-element.47, f32[10,34,258]{2,1,0:T(8,128)S(1)} %get-tuple-element.29, ...), kind=kLoop, calls=%fused_computation.127 | loop fusion | flops 23068672 | bytes 4194304 | tf_op jit(solution)/shard_map/broadcast_in_dim | solution.py:129
  80.3 3.5 %collective-permute-start.6 = (f32[4,2,32,256]{3,2,1,0:T(8,128)}, f32[4,2,32,256]{3,2,1,0:T(8,128)S(1)}, u32[]{:S(2)}, u32[]{:S(2)}) collective-permute-start(f32[4,2,32,256]{3,2,1,0:T(8,128)} %get-tuple-element.64), channel_id=1, source_target_pairs={{0,4},{4,8},{8,12},{1,5},{5,9},{9,13},{2,6},{6,10},{10,14},{3,7},{... | collective-permute-start | bytes 786440 | tf_op jit(solution)/shard_map/ppermute | solution.py:22
  85.6 4.4 %collective-permute-done.6 = f32[4,2,32,256]{3,2,1,0:T(8,128)S(1)} collective-permute-done((f32[4,2,32,256]{3,2,1,0:T(8,128)}, f32[4,2,32,256]{3,2,1,0:T(8,128)S(1)}, u32[]{:S(2)}, u32[]{:S(2)}) %collective-permute-start.6) | collective-permute-done | bytes 262176 | tf_op jit(solution)/shard_map/ppermute | solution.py:22
  90.0 4.7 %collective-permute-done.7 = f32[4,2,32,256]{3,2,1,0:T(8,128)} collective-permute-done((f32[4,2,32,256]{3,2,1,0:T(8,128)}, f32[4,2,32,256]{3,2,1,0:T(8,128)}, u32[]{:S(2)}, u32[]{:S(2)}) %collective-permute-start.7) | collective-permute-done | bytes 262176 | tf_op jit(solution)/shard_map/ppermute | solution.py:25
  99.9 4.1 %collective-permute-done.9 = f32[4,12,2,256]{3,2,1,0:T(2,128)S(1)} collective-permute-done((f32[4,12,2,256]{3,2,1,0:T(2,128)S(1)}, f32[4,12,2,256]{3,2,1,0:T(2,128)S(1)}, u32[]{:S(2)}, u32[]{:S(2)}) %collective-permute-start.9) | collective-permute-done | bytes 98336 | tf_op jit(solution)/shard_map/ppermute | solution.py:25
  110.7 2.2 %copy.29 = f32[4,12,36,2]{2,0,3,1:T(4,128)} copy(f32[4,12,36,2]{3,2,1,0:T(8,128)} %get-tuple-element.53) | data formatting | bytes 27648 | tf_op jit(solution)/shard_map/slice | solution.py:25
  116.8 2.2 %copy.30 = f32[4,12,36,2]{3,2,1,0:T(8,128)} copy(f32[4,12,36,2]{2,0,3,1:T(4,128)} %collective-permute-done.10) | data formatting | bytes 27648 | tf_op jit(solution)/shard_map/ppermute | solution.py:22
  119.1 2.2 %copy.31 = f32[4,12,36,2]{3,2,1,0:T(8,128)} copy(f32[4,12,36,2]{2,0,3,1:T(4,128)} %collective-permute-done.11) | data formatting | bytes 27648 | tf_op jit(solution)/shard_map/ppermute | solution.py:25
  121.2 3.3 %pad_maximum_fusion.1 = f32[4,12,36,260]{3,2,1,0:T(8,128)S(1)} fusion(f32[4,12,36,2]{3,2,1,0:T(8,128)} %copy.31, f32[4,12,2,256]{3,2,1,0:T(2,128)} %copy-done.12, f32[4,2,32,256]{3,2,1,0:T(8,128)} %collective-permute-done.7, f32[1,8,32,256]{3,2,1,0:T(8,128)S(1)} %fusion.51, f32[3,8,32,256]{3,2,1,0:T(8,128)} %copy-done.2, ...), kind=kLoop, calls=%fused_computation.4 | loop fusion | flops 3144960 | bytes 3594240 | tf_op jit(solution)/shard_map/concatenate | solution.py:26
  124.8 3.8 %multiply_multiply_fusion.2 = (f32[10,34,258]{2,1,0:T(8,128)S(1)}, f32[10,34,258]{2,1,0:T(8,128)}, f32[10,34,258]{2,1,0:T(8,128)S(1)}, f32[10,34,258]{2,1,0:T(8,...) fusion(f32[12,36,260]{2,1,0:T(8,128)S(1)} %get-tuple-element.33, ...), kind=kLoop, calls=%fused_computation.61 | loop fusion | flops 2456160 | bytes 8421120 | tf_op jit(solution)/shard_map/mul | solution.py:107
  128.6 2.1 %multiply_multiply_fusion = (f32[10,34,258]{2,1,0:T(8,128)S(1)}, f32[10,34,258]{2,1,0:T(8,128)}, f32[10,34,258]{2,1,0:T(8,128)S(1)}, f32[10,34,258]{2,1,0:T(8,128)S(1)}) fusion(f32[12,36,260]{2,1,0:T(8,128)S(1)} %get-tuple-element.33, f32[12,36,260]{2,1,0:T(8,128)S(1)} %get-tuple-element.30, f32[12,36,260]{2,1,0:T(8,128)S(1)} %get-tuple-element.31, ...), kind=kLoop, calls=%fused_computation.58 | loop fusion | flops 1666680 | bytes 4912320 | tf_op jit(solution)/shard_map/mul | solution.py:107
  134.8 13.5 %psum.14 = f32[3,4096]{1,0:T(4,128)} all-reduce(f32[3,4096]{1,0:T(4,128)} %fusion), channel_id=1, replica_groups=mesh['groups'=2,'slab'=4,'pencil'=2,'comp'=2] {'pencil','comp'}, use_global_device_ids=true, to_apply=%region_1.0 | all-reduce | flops 12288 | bytes 98304 | tf_op jit(solution)/shard_map/psum | solution.py:145
  148.3 19.0 %psum.15 = f32[3,4096]{1,0:T(4,128)} all-reduce(f32[3,4096]{1,0:T(4,128)} %psum.14), channel_id=1, replica_groups=mesh['groups'=2,'slab'=4,'pencil'=2,'comp'=2] {'slab'}, use_global_device_ids=true, to_apply=%region_2.0 | all-reduce | flops 12288 | bytes 98304 | tf_op jit(solution)/shard_map/psum | solution.py:145
  167.3 31.0 %fusion.26 = f32[8,32,256]{2,1,0:T(8,128)} fusion(f32[8,32,256]{2,1,0:T(8,128)} %param.6, f32[12,36,260]{2,1,0:T(8,128)S(1)} %copy-done.4, f32[10,34,258]{2,1,0:T(8,128)S(1)} %get-tuple-element.39, f32[10,34,258]{2,1,0:T(8,128)} %get-tuple-element.40, f32[10,34,258]{2,1,0:T(8,128)} %get-tuple-element.18, f32[10,34,258]{2,1,0:T(8,128)} %get-tuple-element.44, ...), kind=kLoop, calls=%fused_computation.82 | loop fusion | flops 23068672 | bytes 4194304 | tf_op jit(solution)/shard_map/add | solution.py:116
  (75 shorter events, 39.0 us)
Async XLA Ops:
  0.6 132.4 %copy-start = (bf16[8,32,1,4096]{3,1,2,0:T(8,128)(2,1)S(1)}, bf16[8,32,1,4096]{3,1,2,0:T(8,128)(2,1)}, u32[]{:S(2)}) copy-start(bf16[8,32,1,4096]{3,1,2,0:T(8,128)(2,1)} %param.8) | copy-start | bytes 6291460
  0.6 28.0 %copy-start.1 = (f32[3,8,32,256]{3,2,1,0:T(8,128)S(1)}, f32[3,8,32,256]{3,2,1,0:T(8,128)}, u32[]{:S(2)}) copy-start(f32[3,8,32,256]{3,2,1,0:T(8,128)} %param.5) | copy-start | bytes 2359300
  2.9 10.5 %collective-permute-start = (f32[4,2,32,256]{3,2,1,0:T(8,128)S(1)}, f32[4,2,32,256]{3,2,1,0:T(8,128)S(1)}, u32[]{:S(2)}, u32[]{:S(2)}) collective-permute-start(f32[4,2,32,256]{3,2,1,0:T(8,128)S(1)} %get-tuple-element.66), channel_id=1, source_target_pairs={{0,4},{4,8},{8,12},{1,5},{5,9},{9,13},{2,6},{6,10},{10,14},{3,7},{... | collective-permute-start | bytes 786440 | tf_op jit(solution)/shard_map/ppermute | solution.py:22
  7.8 9.7 %collective-permute-start.1 = (f32[4,2,32,256]{3,2,1,0:T(8,128)S(1)}, f32[4,2,32,256]{3,2,1,0:T(8,128)S(1)}, u32[]{:S(2)}, u32[]{:S(2)}) collective-permute-start(f32[4,2,32,256]{3,2,1,0:T(8,128)S(1)} %get-tuple-element.67), channel_id=1, source_target_pairs={{4,0},{8,4},{12,8},{5,1},{9,5},{13,9},{6,2},{10,6},{14,10},{7,3},{... | collective-permute-start | bytes 786440 | tf_op jit(solution)/shard_map/ppermute | solution.py:25
  17.5 13.0 %copy-start.5 = (f32[4,2,32,256]{3,2,1,0:T(8,128)}, f32[4,2,32,256]{3,2,1,0:T(8,128)S(1)}, u32[]{:S(2)}) copy-start(f32[4,2,32,256]{3,2,1,0:T(8,128)S(1)} %collective-permute-done.1) | copy-start | bytes 786436
  18.7 5.6 %collective-permute-start.2 = (f32[4,12,2,256]{3,2,1,0:T(2,128)S(1)}, f32[4,12,2,256]{3,2,1,0:T(2,128)S(1)}, u32[]{:S(2)}, u32[]{:S(2)}) collective-permute-start(f32[4,12,2,256]{3,2,1,0:T(2,128)S(1)} %get-tuple-element.58), channel_id=1, source_target_pairs={{0,2},{1,3},{4,6},{5,7},{8,10},{9,11},{12,14},{13,15},{16,18},{17,... | collective-permute-start | bytes 294920 | tf_op jit(solution)/shard_map/ppermute | solution.py:22
  22.1 6.5 %collective-permute-start.3 = (f32[4,12,2,256]{3,2,1,0:T(2,128)S(1)}, f32[4,12,2,256]{3,2,1,0:T(2,128)S(1)}, u32[]{:S(2)}, u32[]{:S(2)}) collective-permute-start(f32[4,12,2,256]{3,2,1,0:T(2,128)S(1)} %get-tuple-element.59), channel_id=1, source_target_pairs={{2,0},{3,1},{6,4},{7,5},{10,8},{11,9},{14,12},{15,13},{18,16},{19,... | collective-permute-start | bytes 294920 | tf_op jit(solution)/shard_map/ppermute | solution.py:25
  28.6 1.9 copy-start.13
  32.1 5.4 %collective-permute-start.4 = (f32[4,12,36,2]{2,0,3,1:T(4,128)S(1)}, f32[4,12,36,2]{2,0,3,1:T(4,128)}, u32[]{:S(2)}, u32[]{:S(2)}) collective-permute-start(f32[4,12,36,2]{2,0,3,1:T(4,128)S(1)} %copy.24), channel_id=1, source_target_pairs={{0,1},{2,3},{4,5},{6,7},{8,9},{10,11},{12,13},{14,15},{16,17},{18,... | collective-permute-start | bytes 41480 | tf_op jit(solution)/shard_map/ppermute | solution.py:22
  36.3 3.5 %collective-permute-start.5 = (f32[4,12,36,2]{2,0,3,1:T(4,128)}, f32[4,12,36,2]{2,0,3,1:T(4,128)}, u32[]{:S(2)}, u32[]{:S(2)}) collective-permute-start(f32[4,12,36,2]{2,0,3,1:T(4,128)} %copy.25), channel_id=1, source_target_pairs={{1,0},{3,2},{5,4},{7,6},{9,8},{11,10},{13,12},{15,14},{17,16},{19,... | collective-permute-start | bytes 41480 | tf_op jit(solution)/shard_map/ppermute | solution.py:25
  49.9 29.5 %copy-start.6 = (f32[1,8,32,256]{3,2,1,0:T(8,128)}, f32[1,8,32,256]{3,2,1,0:T(8,128)S(1)}, u32[]{:S(2)}) copy-start(f32[1,8,32,256]{3,2,1,0:T(8,128)S(1)} %get-tuple-element.71) | copy-start | bytes 786436
  49.9 29.5 %copy-start.8 = (f32[1,8,32,256]{3,2,1,0:T(8,128)}, f32[1,8,32,256]{3,2,1,0:T(8,128)S(1)}, u32[]{:S(2)}) copy-start(f32[1,8,32,256]{3,2,1,0:T(8,128)S(1)} %get-tuple-element.72) | copy-start | bytes 786436
  49.9 29.5 %copy-start.10 = (f32[1,8,32,256]{3,2,1,0:T(8,128)}, f32[1,8,32,256]{3,2,1,0:T(8,128)S(1)}, u32[]{:S(2)}) copy-start(f32[1,8,32,256]{3,2,1,0:T(8,128)S(1)} %get-tuple-element.73) | copy-start | bytes 786436
  50.1 30.2 %copy-start.2 = (f32[3,8,32,256]{3,2,1,0:T(8,128)}, f32[3,8,32,256]{3,2,1,0:T(8,128)S(1)}, u32[]{:S(2)}) copy-start(f32[3,8,32,256]{3,2,1,0:T(8,128)S(1)} %fusion.4) | copy-start | bytes 2359300
  80.3 9.7 %collective-permute-start.6 = (f32[4,2,32,256]{3,2,1,0:T(8,128)}, f32[4,2,32,256]{3,2,1,0:T(8,128)S(1)}, u32[]{:S(2)}, u32[]{:S(2)}) collective-permute-start(f32[4,2,32,256]{3,2,1,0:T(8,128)} %get-tuple-element.64), channel_id=1, source_target_pairs={{0,4},{4,8},{8,12},{1,5},{5,9},{9,13},{2,6},{6,10},{10,14},{3,7},{... | collective-permute-start | bytes 786440 | tf_op jit(solution)/shard_map/ppermute | solution.py:22
  83.8 10.9 %collective-permute-start.7 = (f32[4,2,32,256]{3,2,1,0:T(8,128)}, f32[4,2,32,256]{3,2,1,0:T(8,128)}, u32[]{:S(2)}, u32[]{:S(2)}) collective-permute-start(f32[4,2,32,256]{3,2,1,0:T(8,128)} %get-tuple-element.65), channel_id=1, source_target_pairs={{4,0},{8,4},{12,8},{5,1},{9,5},{13,9},{6,2},{10,6},{14,10},{7,3},{... | collective-permute-start | bytes 786440 | tf_op jit(solution)/shard_map/ppermute | solution.py:25
  95.8 4.1 %collective-permute-start.8 = (f32[4,12,2,256]{3,2,1,0:T(2,128)S(1)}, f32[4,12,2,256]{3,2,1,0:T(2,128)S(1)}, u32[]{:S(2)}, u32[]{:S(2)}) collective-permute-start(f32[4,12,2,256]{3,2,1,0:T(2,128)S(1)} %get-tuple-element.56), channel_id=1, source_target_pairs={{0,2},{1,3},{4,6},{5,7},{8,10},{9,11},{12,14},{13,15},{16,18},{17,... | collective-permute-start | bytes 294920 | tf_op jit(solution)/shard_map/ppermute | solution.py:22
  97.4 6.7 %collective-permute-start.9 = (f32[4,12,2,256]{3,2,1,0:T(2,128)S(1)}, f32[4,12,2,256]{3,2,1,0:T(2,128)S(1)}, u32[]{:S(2)}, u32[]{:S(2)}) collective-permute-start(f32[4,12,2,256]{3,2,1,0:T(2,128)S(1)} %get-tuple-element.57), channel_id=1, source_target_pairs={{2,0},{3,1},{6,4},{7,5},{10,8},{11,9},{14,12},{15,13},{18,16},{19,... | collective-permute-start | bytes 294920 | tf_op jit(solution)/shard_map/ppermute | solution.py:25
  104.0 3.1 %copy-start.12 = (f32[4,12,2,256]{3,2,1,0:T(2,128)}, f32[4,12,2,256]{3,2,1,0:T(2,128)S(1)}, u32[]{:S(2)}) copy-start(f32[4,12,2,256]{3,2,1,0:T(2,128)S(1)} %collective-permute-done.9) | copy-start | bytes 294916
  108.8 8.1 %collective-permute-start.10 = (f32[4,12,36,2]{2,0,3,1:T(4,128)S(1)}, f32[4,12,36,2]{2,0,3,1:T(4,128)}, u32[]{:S(2)}, u32[]{:S(2)}) collective-permute-start(f32[4,12,36,2]{2,0,3,1:T(4,128)S(1)} %copy.28), channel_id=1, source_target_pairs={{0,1},{2,3},{4,5},{6,7},{8,9},{10,11},{12,13},{14,15},{16,17},{18,... | collective-permute-start | bytes 41480 | tf_op jit(solution)/shard_map/ppermute | solution.py:22
  112.9 6.1 %collective-permute-start.11 = (f32[4,12,36,2]{2,0,3,1:T(4,128)}, f32[4,12,36,2]{2,0,3,1:T(4,128)}, u32[]{:S(2)}, u32[]{:S(2)}) collective-permute-start(f32[4,12,36,2]{2,0,3,1:T(4,128)} %copy.29), channel_id=1, source_target_pairs={{1,0},{3,2},{5,4},{7,6},{9,8},{11,10},{13,12},{15,14},{17,16},{19,... | collective-permute-start | bytes 41480 | tf_op jit(solution)/shard_map/ppermute | solution.py:25
  124.8 3.8 %copy-start.3 = (f32[12,36,260]{2,1,0:T(8,128)}, f32[12,36,260]{2,1,0:T(8,128)S(1)}, u32[]{:S(2)}) copy-start(f32[12,36,260]{2,1,0:T(8,128)S(1)} %get-tuple-element.33) | copy-start | bytes 1347844
  131.8 1.6 copy-start.14
  132.9 34.3 %copy-start.4 = (f32[12,36,260]{2,1,0:T(8,128)S(1)}, f32[12,36,260]{2,1,0:T(8,128)}, u32[]{:S(2)}) copy-start(f32[12,36,260]{2,1,0:T(8,128)} %copy-done.3) | copy-start | bytes 1347844
  (5 other events, 6.4 us)
